TPU v7x, 32 devices: a whole 2x2x4 slice. The times are simulated.
32 devices in a mesh: tm: 16 (over z, y, x), state: 2 (over core).
Axes of the slice: x: 2, y: 2, z: 4, core: 2. Of those that a mesh axis runs over, the one named last changes fastest.
Arguments:
- symbols: int32 [8], P('state'), may hold values from 0 to 255
- emission: float32 [8192, 256], P('tm'), may hold values from 0.2 to 5
- decay: float32 [2, 8192], P('state', 'tm'), may hold values from 0.05 to 1
- left_factor: float32 [2, 64, 8192], P('state', None, 'tm'), may hold values from 0.1 to 3
- right_factor: float32 [2, 64, 8192], P('state', None, 'tm'), may hold values from 0.001 to 0.03
- initial: float32 [8192], P('tm'), may hold values from 0.1 to 10
Outputs:
- filtered: float32 [8, 8192], P('state', 'tm')
- log_scale: float32 [8], P('state')
All inputs are finite; a program needn't handle non-finite values.
Results may differ from a plain program's by a relative error of at most 0.00011.
Values sent between devices are 32-bit elements; how exact they have to be, the bound alone decides.
No kernel may reach another device: no remote copies, remote signals or barrier semaphores. Data moves between devices by JAX's collectives and lax.ppermute only.
A program may use at most 64 MiB of HBM per device.

v0:
```python
import jax
import jax.numpy as jnp
from jax import lax
from jax.sharding import PartitionSpec as P

S = 8192


PRECISE = lax.Precision.HIGHEST


def passed_along(value, axis, steps):
    count = lax.axis_size(axis)
    first, last = (max(0, -steps), min(count, count - steps))
    return lax.ppermute(value, axis, [(source, source + steps) for source in range(first, last)])


def run_span(entry_vec, emitted_all, decay_row, left_rows, right_rows):
    projected, total_sum = lax.psum(
        (jnp.dot(left_rows, entry_vec, precision=PRECISE), jnp.sum(entry_vec)), "tm"
    )
    rescale = S / total_sum
    belief = entry_vec * rescale
    mixture = projected * rescale / S

    def frame(state_pair, emitted):
        belief_now, mixture_now = state_pair
        unscaled = emitted * (
            decay_row * belief_now + jnp.dot(mixture_now, right_rows, precision=PRECISE)
        )
        proj_next, total_next = lax.psum(
            (jnp.dot(left_rows, unscaled, precision=PRECISE), jnp.sum(unscaled)), "tm"
        )
        normal = total_next / S
        belief_next = unscaled / normal
        mixture_next = proj_next / normal / S
        return ((belief_next, mixture_next), (belief_next, jnp.log(normal)))

    (closing, mixture_end), (beliefs, log_levels) = lax.scan(frame, (belief, mixture), emitted_all)
    return (beliefs, log_levels, closing)


def span_map(emitted_all, decay_row, left_rows, right_rows):
    frames = emitted_all.shape[0]
    rank_cols = left_rows.shape[0]
    cells = left_rows.shape[1]
    growth = emitted_all * decay_row[None, :]
    markers = jnp.eye(frames, dtype=jnp.float32)

    def advance(state_pair, inputs):
        reached, weights = state_pair
        grow_row, emitted, marker = inputs
        weights_next = weights * grow_row[None, :] + marker[:, None] * emitted[None, :]
        return ((reached * grow_row, weights_next), (reached, weights_next))

    begin_pair = (jnp.ones((cells,), jnp.float32), jnp.zeros((frames, cells), jnp.float32))
    (final_reach, final_weights), (reached_all, weights_all) = lax.scan(
        advance, begin_pair, (growth, emitted_all, markers)
    )
    probes = (left_rows[None, :, :] * reached_all[:, None, :]).reshape(
        frames * rank_cols, cells
    ) / S
    vb_rows = right_rows[None, :, :] * final_weights[:, None, :]
    pair_rows = weights_all[: frames - 1].reshape((frames - 1) * frames, cells)
    group_size = max(rank_cols // 8, 1)
    blocks = []
    for offset in range(0, rank_cols, group_size):
        cross_rows = (
            left_rows[offset : offset + group_size, None, :] * right_rows[None, :, :]
        ).reshape(-1, cells)
        blocks.append(jnp.einsum("pw,qw->pq", pair_rows, cross_rows, precision=PRECISE))
    local_terms = jnp.concatenate(blocks, axis=1) / S
    coupling = lax.psum(local_terms, "tm").reshape(frames - 1, frames, rank_cols, rank_cols)
    shifted = jnp.concatenate(
        [jnp.zeros((1, frames, rank_cols, rank_cols), jnp.float32), coupling], axis=0
    )

    def solve_back(turn_index, response):
        column = frames - 1 - turn_index
        factors = lax.dynamic_index_in_dim(shifted, column, 1, keepdims=False)
        coupled = jnp.einsum("kab,kaw->bw", factors, response, precision=PRECISE)
        own_rows = lax.dynamic_index_in_dim(vb_rows, column, 0, keepdims=False)
        return lax.dynamic_update_index_in_dim(response, own_rows + coupled, column, 0)

    response = lax.fori_loop(
        0, frames, solve_back, jnp.zeros((frames, rank_cols, cells), jnp.float32)
    )
    return (probes, final_reach, response)


def per_device(symbols, emission, decay, left_factor, right_factor, initial):
    decay_row = decay[0]
    left_rows = left_factor[0]
    right_rows = right_factor[0]
    onehot = (symbols[:, None] == jnp.arange(emission.shape[1], dtype=jnp.int32)[None, :]).astype(
        jnp.float32
    )
    emitted_all = jnp.einsum("fv,sv->fs", onehot, emission, precision=PRECISE)
    leader = lax.axis_index("state") == 0

    def pass_on(closing):
        return jnp.where(leader, initial, passed_along(closing, "state", 1))

    probes, final_reach, response = span_map(emitted_all, decay_row, left_rows, right_rows)
    frames = emitted_all.shape[0]
    rank_cols = left_rows.shape[0]

    def section(step_idx, entry_vec):
        projected, total_sum = lax.psum(
            (jnp.dot(probes, entry_vec, precision=PRECISE), jnp.sum(entry_vec)), "tm"
        )
        rescale = S / total_sum
        carried = jnp.einsum(
            "ka,kaw->w",
            (projected * rescale).reshape(frames, rank_cols),
            response,
            precision=PRECISE,
        )
        return pass_on(final_reach * entry_vec * rescale + carried)

    entry_vec = lax.fori_loop(0, lax.axis_size("state") - 1, section, initial)
    beliefs, log_levels, closing = run_span(
        entry_vec, emitted_all, decay_row, left_rows, right_rows
    )
    return (beliefs, log_levels)


def solution(mesh):
    return jax.shard_map(
        per_device,
        mesh=mesh,
        in_specs=(
            P("state"),
            P("tm", None),
            P("state", "tm"),
            P("state", None, "tm"),
            P("state", None, "tm"),
            P("tm"),
        ),
        out_specs=(P("state", "tm"), P("state")),
        check_vma=False,
    )
```

profile of v0, /device:TPU:0, one launch (start us, length us, event | category | flops | bytes accessed | tf_op | source)
XLA Modules:
  0.0 347.2 jit_solution(12387997942848952314)
XLA Ops:
  7.3 0.9 slice_bitcast_fusion
  9.3 0.8 while.54
  10.2 1.1 broadcast_multiply_fusion
  11.3 1.0 convolution_dynamic-update-slice_fusion.7
  12.2 1.0 convolution_dynamic-update-slice_fusion.6
  13.2 1.0 convolution_dynamic-update-slice_fusion.5
  14.2 1.0 convolution_dynamic-update-slice_fusion.4
  15.2 1.0 convolution_dynamic-update-slice_fusion.3
  16.1 1.0 convolution_dynamic-update-slice_fusion.2
  17.1 1.0 convolution_dynamic-update-slice_fusion.1
  18.1 1.0 convolution_dynamic-update-slice_fusion
  19.3 0.9 copy.8
  20.2 0.9 copy-done.1
  22.9 44.2 %all-reduce.3 = (f32[256]{0:T(256)S(1)}, f32[]{:T(128)}) all-reduce(f32[256]{0:T(256)S(1)} %bitcast.161, f32[]{:T(128)} %reduce_sum.28), channel_id=1, replica_groups=mesh['tm'=16,'state'=2] {'tm'}, use_global_device_ids=true, to_apply=%region_4.5 | all-reduce | flops 257 | bytes 2056 | tf_op jit(solution)/shard_map/while/body/eval_jaxpr/psum | solution.py:109
  67.9 63.9 %all-reduce.8.cloned.1.call-done = f32[3,4,64,64]{2,3,0,1:T(8,128)} async-done(((f32[3,4,64,64]{2,3,0,1:T(8,128)}), f32[3,4,64,64]{2,3,0,1:T(8,128)}) %all-reduce.8.cloned.1.call-update) | async-done | bytes 196624 | tf_op jit(solution)/shard_map/psum | solution.py:73
  131.8 1.0 concatenate.7
  132.9 2.0 while.52
  135.3 1.3 collective-permute-start
  138.2 40.5 %all-reduce.2 = (f32[]{:T(128)}, f32[64]{0:T(128)S(1)}) all-reduce(f32[]{:T(128)} %get-tuple-element.314, f32[64]{0:T(128)S(1)} %convolution_bitcast_fusion.2), channel_id=1, replica_groups=mesh['tm'=16,'state'=2] {'tm'}, use_global_device_ids=true, to_apply=%region_9.10 | all-reduce | flops 65 | bytes 520 | tf_op jit(solution)/shard_map/psum | solution.py:19
  179.4 160.4 %while.53 = (s32[]{:T(128)}, f32[512]{0:T(512)S(1)}, f32[64]{0:T(128)S(1)}, f32[4,512]{1,0:T(4,128)S(1)}, f32[4]{0:T(128)S(1)}, /*index=5*/f32[4,512]{1,0:T(4,12...) while((s32[]{:T(128)}, f32[512]{0:T(512)S(1)}, ...), condition=%wide.region_15.16_spmd, body=%wide.region_11.15_spmd.sunk | while | flops 789187 | bytes 290481 | solution.py:39
  180.4 37.2 %all-reduce.5 = (f32[]{:T(128)}, f32[64]{0:T(128)S(1)}) all-reduce(f32[]{:T(128)} %get-tuple-element.468, f32[64]{0:T(128)S(1)} %convolution_bitcast_fusion.4), channel_id=1, replica_groups=mesh['tm'=16,'state'=2] {'tm'}, use_global_device_ids=true, to_apply=%region_13.13 | all-reduce | flops 65 | bytes 520 | tf_op jit(solution)/shard_map/while/body/eval_jaxpr/psum | solution.py:31
  219.5 39.2 %all-reduce.5 = (f32[]{:T(128)}, f32[64]{0:T(128)S(1)}) all-reduce(f32[]{:T(128)} %get-tuple-element.468, f32[64]{0:T(128)S(1)} %convolution_bitcast_fusion.4), channel_id=1, replica_groups=mesh['tm'=16,'state'=2] {'tm'}, use_global_device_ids=true, to_apply=%region_13.13 | all-reduce | flops 65 | bytes 520 | tf_op jit(solution)/shard_map/while/body/eval_jaxpr/psum | solution.py:31
  260.5 37.3 %all-reduce.5 = (f32[]{:T(128)}, f32[64]{0:T(128)S(1)}) all-reduce(f32[]{:T(128)} %get-tuple-element.468, f32[64]{0:T(128)S(1)} %convolution_bitcast_fusion.4), channel_id=1, replica_groups=mesh['tm'=16,'state'=2] {'tm'}, use_global_device_ids=true, to_apply=%region_13.13 | all-reduce | flops 65 | bytes 520 | tf_op jit(solution)/shard_map/while/body/eval_jaxpr/psum | solution.py:31
  299.7 39.2 %all-reduce.5 = (f32[]{:T(128)}, f32[64]{0:T(128)S(1)}) all-reduce(f32[]{:T(128)} %get-tuple-element.468, f32[64]{0:T(128)S(1)} %convolution_bitcast_fusion.4), channel_id=1, replica_groups=mesh['tm'=16,'state'=2] {'tm'}, use_global_device_ids=true, to_apply=%region_13.13 | all-reduce | flops 65 | bytes 520 | tf_op jit(solution)/shard_map/while/body/eval_jaxpr/psum | solution.py:31
  (103 shorter events, 13.0 us)
Async XLA Ops:
  7.2 1.2 copy-start
  7.2 124.7 %all-reduce.8.cloned.1.call-start = ((), (), s32[]{:S(2)}) async-start(), calls=%async_computation | async-start | bytes 786432 | tf_op jit(solution)/shard_map/psum | solution.py:73
  8.2 0.7 copy-start.3
  8.2 0.7 copy-start.6
  9.2 0.9 copy-start.2
  20.2 0.9 copy-start.1
  21.1 0.7 copy-start.4
  135.3 2.1 collective-permute-start
  339.8 0.5 copy-start.7
  339.8 0.6 copy-start.5
Sparse Core Ops, SparseCore 0:
  20.3 111.4 all-reduce.7
where the time goes:
time: 348 us; the launch traced here: 347 us
  blocking collectives  238 us (68%)
  waiting for transfers between devices  64.7 us (19%)
  between operations  15.6 us (4%)
  matrix products  12.4 us (4%)
  local copies, waits for them, and re-layouts  7.07 us (2%)
  other arithmetic  5.31 us (2%)
    psum x4, blocking collectives, frame(): lax.psum((jnp.dot(left_rows, unscaled, precision=PRECISE), jnp.sum(unscal...  153 us
    psum x1, waiting for transfers between devices, span_map(): lax.psum(local_terms, 'tm')  63.9 us
    psum x1, blocking collectives, section(): lax.psum((jnp.dot(probes, entry_vec, precision=PRECISE), jnp.sum(entry_ve...  44.2 us
    psum x1, blocking collectives, run_span(): lax.psum((jnp.dot(left_rows, entry_vec, precision=PRECISE), jnp.sum(entry...  40.5 us
    dot_general x8, matrix products, span_map(): jnp.einsum('pw,qw->pq', pair_rows, cross_rows, precision=PRECISE)  7.79 us
  transfers between devices with their start and end apart: 2, of which 2 were waited for; matrix products, arithmetic and copies ran while one was open for 0% of the time, Pallas kernels for 0%

commit v1 on v0

v1 whole, which is shorter than its diff:
```python
import jax
import jax.numpy as jnp
from jax import lax
from jax.experimental import pallas as pl
from jax.experimental.pallas import tpu as pltpu
from jax.sharding import PartitionSpec as P

PRECISE = lax.Precision.HIGHEST
LANES = (((1,), (1,)), ((), ()))
VMEM = pl.BlockSpec(memory_space=pltpu.VMEM)
SMEM = pl.BlockSpec(memory_space=pltpu.SMEM)


def up(count, step):
    return -(-count // step) * step


def dot_lanes(rows, weights):
    return lax.dot_general(
        rows, weights, LANES, precision=PRECISE, preferred_element_type=jnp.float32
    )


def halves(value):
    top = value.astype(jnp.bfloat16)
    return top, (value - top.astype(jnp.float32)).astype(jnp.bfloat16)


def dot_split(rows, weights):
    (row_top, row_low), (top, low) = halves(rows), halves(weights)

    def part(left, right):
        return lax.dot_general(left, right, LANES, preferred_element_type=jnp.float32)

    return part(row_top, top) + (part(row_top, low) + part(row_low, top))


class Plan:
    def __init__(self, frames, rank, members):
        self.frames, self.rank = frames, rank
        self.share = frames // 2
        self.own = [(s, t) for t in range(1, frames) for s in range(t)]
        self.cross = [(s, j) for j in range(self.share) for s in range(frames)]
        self.pairs = len(self.own) + len(self.cross)
        self.tiles = (self.pairs + 1) // 2
        self.levels = [(s, t) for t in range(1, frames + 1) for s in range(t)]
        at = self.tiles * rank
        self.entry_at, at = at, at + up(frames, 8)
        self.own_at, at = at, at + up(len(self.levels), 8)
        self.cross_at, at = at, at + up(len(self.cross), 8)
        self.sum_at, at = at, at + up(frames + 1, 8)
        self.used = at
        self.rows = up(at, 8 * members)
        self.chunk = self.rows // members


def chain(emitted, growth, frames):
    weights = {}
    for s in range(frames):
        weights[s, s + 1] = emitted[s]
        for t in range(s + 2, frames + 1):
            weights[s, t] = weights[s, t - 1] * growth[t - 1]
    reach = [jnp.ones_like(emitted[0])]
    for t in range(frames):
        reach.append(reach[-1] * growth[t])
    return weights, reach


def stack_rows(rows):
    filler = up(len(rows), 8) - len(rows)
    return jnp.concatenate(list(rows) + [jnp.zeros_like(rows[0])] * filler, axis=0)


def both_blocks(first, own, other, rank, frames):
    own_e = [own[rank + f : rank + f + 1] for f in range(frames)]
    other_e = [other[rank + f : rank + f + 1] for f in range(frames)]
    own_d = own[rank + frames : rank + frames + 1]
    other_d = other[rank + frames : rank + frames + 1]
    blocks = []
    for lead in (True, False):
        pick = first if lead else jnp.logical_not(first)
        e = [jnp.where(pick, a, b) for a, b in zip(own_e, other_e)]
        d = jnp.where(pick, own_d, other_d)
        blocks.append((e, d))
    return own_e, own_d, blocks


def offer_kernel(place, symbols, emission, decay, left, right, out):
    frames = symbols.shape[0]
    rank, cells = left.shape
    pad = up(frames, 8)
    at = lax.broadcasted_iota(jnp.int32, (pad, emission.shape[1]), 0)
    lane = lax.broadcasted_iota(jnp.int32, (pad, emission.shape[1]), 1)
    wanted = jnp.full(at.shape, -1, jnp.int32)
    for f in range(frames):
        wanted = jnp.where(at == f, symbols[f], wanted)
    onehot = (lane == wanted).astype(jnp.float32)
    emitted = dot_lanes(onehot, emission[...])
    out[:rank] = jnp.where(place[0] == 0, right[...], left[...])
    rest = [emitted[:frames], decay[...]]
    spare = out.shape[0] - rank - frames - 1
    if spare:
        rest.append(jnp.zeros((spare, cells), jnp.float32))
    out[rank:] = jnp.concatenate(rest, axis=0)


def partial_kernel(plan, place, own_ref, other_ref, left, right, entry, out):
    frames, rank = plan.frames, plan.rank
    first = place[0] == 0
    own_e, own_d, ((e0, d0), (e1, d1)) = both_blocks(
        first, own_ref[rank:], other_ref[rank:], 0, frames
    )
    left_own, right_own = left[...], right[...]
    left_late = jnp.where(first, other_ref[:rank], left_own)
    right_early = jnp.where(first, right_own, other_ref[:rank])
    start = entry[...]
    w_own, _ = chain(own_e, [e * own_d for e in own_e], frames)
    w0, reach0 = chain(e0, [e * d0 for e in e0], frames)
    _, reach1 = chain(e1, [e * d1 for e in e1], frames)
    share = plan.share
    shift = [jnp.where(first, reach1[j], reach1[j + share]) for j in range(share + 1)]
    arrive = [
        start * jnp.where(first, reach0[t], reach0[frames] * reach1[t]) for t in range(frames + 1)
    ]
    own_rows = [right_own * w_own[pair] for pair in plan.own] + [stack_rows(arrive[:frames])]
    cross_w = [w0[s, frames] * shift[j] for s, j in plan.cross]
    cross_rows = [right_early * w for w in cross_w]
    mapped_own = dot_split(jnp.concatenate(own_rows, axis=0), left_own)
    mapped_cross = dot_split(jnp.concatenate(cross_rows, axis=0), left_late)
    many = len(plan.own)
    blocks = [mapped_own[k * rank : (k + 1) * rank] for k in range(many)]
    blocks += [mapped_cross[k * rank : (k + 1) * rank] for k in range(len(plan.cross))]
    if len(blocks) % 2:
        blocks.append(jnp.zeros_like(blocks[0]))
    for k in range(plan.tiles):
        out[k * rank : (k + 1) * rank] = jnp.concatenate(
            [blocks[k], blocks[plan.tiles + k]], axis=1
        )

    def put(at, value):
        out[at : at + value.shape[0]] = jnp.concatenate([value, jnp.zeros_like(value)], axis=1)

    put(plan.entry_at, mapped_own[many * rank :])
    put(plan.own_at, dot_lanes(stack_rows([w_own[pair] for pair in plan.levels]), right_own))
    later = [w0[s, frames] * shift[j + 1] for s, j in plan.cross]
    put(plan.cross_at, dot_lanes(stack_rows(later), right_early))
    totals = jnp.sum(stack_rows(arrive[1:] + [start]), axis=1, keepdims=True)
    out[plan.sum_at : plan.used] = jnp.broadcast_to(totals, (totals.shape[0], out.shape[1]))
    if plan.rows > plan.used:
        out[plan.used :] = jnp.zeros((plan.rows - plan.used, out.shape[1]), jnp.float32)


def solve_kernel(plan, states, place, total, own_ref, other_ref, right, entry, out, logs):
    frames, rank, share, chunk = plan.frames, plan.rank, plan.share, plan.chunk
    first = place[0] == 0
    width = total.shape[3]
    count = 2 * frames

    def rows(core, at, size):
        if at % chunk == 0 and size % chunk == 0:
            return total[at // chunk : (at + size) // chunk, core].reshape(size, width)
        return jnp.concatenate(
            [total[r // chunk, core, r % chunk : r % chunk + 8] for r in range(at, at + size, 8)],
            axis=0,
        )

    lane = lax.broadcasted_iota(jnp.int32, (1, width), 1)
    low = lane < rank
    row_of = lax.broadcasted_iota(jnp.int32, (rank, width), 0)
    lane_of = lax.broadcasted_iota(jnp.int32, (rank, width), 1)
    diagonal = (lane_of == row_of) | (lane_of == row_of + rank)

    feeds = {s: [] for s in range(count)}
    for core in range(2):
        spans = [(core * frames + s, core * frames + t) for s, t in plan.own]
        spans += [(s, frames + core * share + j) for s, j in plan.cross]
        for k, (s, t) in enumerate(spans):
            feeds[s].append((core, k % plan.tiles, k < plan.tiles, t))

    entries = [rows(core, plan.entry_at, up(frames, 8)) for core in range(2)]
    acc = [entries[t // frames][t % frames : t % frames + 1] for t in range(count)]
    cols, lines = [], []
    for s in range(count):
        line = acc[s] * (1.0 / states)
        cols.append(jnp.sum(jnp.where(diagonal, line, 0.0), axis=1, keepdims=True))
        lines.append(jnp.where(low, line + pltpu.roll(line, rank, 1), 0.0))
        for core, tile, lower, t in feeds[s]:
            gain = jnp.sum(rows(core, tile * rank, rank) * cols[s], axis=0, keepdims=True)
            acc[t] = acc[t] + jnp.where(low if lower else ~low, gain, 0.0)

    level_rows = [jnp.zeros((1, width), jnp.float32) for _ in range(count)]
    for core in range(2):
        weights = rows(core, plan.own_at, up(len(plan.levels), 8))
        for k, (s, t) in enumerate(plan.levels):
            at = core * frames + t - 1
            level_rows[at] = level_rows[at] + weights[k : k + 1] * lines[core * frames + s]
        weights = rows(core, plan.cross_at, up(len(plan.cross), 8))
        for k, (s, j) in enumerate(plan.cross):
            at = frames + core * share + j
            level_rows[at] = level_rows[at] + weights[k : k + 1] * lines[s]
    totals = [rows(core, plan.sum_at, up(frames + 1, 8)) for core in range(2)]
    base = jnp.concatenate(
        [totals[0][frames : frames + 1], totals[0][:frames], totals[1][:frames]], axis=0
    )
    mixed = jnp.sum(jnp.concatenate(level_rows, axis=0), axis=1, keepdims=True)
    levels = [base[:1]] + [base[t + 1 : t + 2] + mixed[t : t + 1] for t in range(count)]

    own_e, own_d, ((e0, d0), (e1, d1)) = both_blocks(
        first, own_ref[rank:], other_ref[rank:], 0, frames
    )
    right_own = right[...]
    right_early = jnp.where(first, right_own, other_ref[:rank])
    belief = entry[...]
    found = []
    for t in range(count):
        e, d = (e0[t], d0) if t < frames else (e1[t - frames], d1)
        factor = right_early if t < frames else right_own
        belief = e * (d * belief + jnp.sum(factor * cols[t], axis=0, keepdims=True))
        found.append(belief)
    for f in range(frames):
        scale = jnp.where(first, levels[f + 1], levels[frames + f + 1])[:, :1]
        before = jnp.where(first, levels[f], levels[frames + f])
        after = jnp.where(first, levels[f + 1], levels[frames + f + 1])
        out[f : f + 1] = jnp.where(first, found[f], found[frames + f]) * (states / scale)
        logs[f : f + 1] = jnp.log(after / before)


def solution(mesh):
    members = mesh.shape["tm"]
    cores = mesh.shape["state"]
    assert cores == 2

    def per_device(symbols, emission, decay, left_factor, right_factor, initial):
        left, right = left_factor[0], right_factor[0]
        frames = symbols.shape[0]
        rank, cells = left.shape
        states = members * cells
        plan = Plan(frames, rank, members)
        width = 2 * rank
        place = lax.axis_index("state").astype(jnp.int32).reshape(1)
        entry = initial.reshape(1, cells)
        offered = pl.pallas_call(
            offer_kernel,
            out_shape=jax.ShapeDtypeStruct((up(rank + frames + 1, 8), cells), jnp.float32),
            in_specs=[SMEM, SMEM, VMEM, VMEM, VMEM, VMEM],
            out_specs=VMEM,
            name="offer",
        )(place, symbols, emission, decay, left, right)
        other = lax.ppermute(offered, "state", [(0, 1), (1, 0)])
        partial = pl.pallas_call(
            lambda *refs: partial_kernel(plan, *refs),
            out_shape=jax.ShapeDtypeStruct((plan.rows, width), jnp.float32),
            in_specs=[SMEM] + [VMEM] * 5,
            out_specs=VMEM,
            name="partial",
        )(place, offered, other, left, right, entry)
        parts = lax.all_to_all(partial, "tm", 0, 0, tiled=True)
        mine = jnp.sum(parts.reshape(members, plan.chunk, width), axis=0)
        copies = jnp.broadcast_to(mine[None], (members * cores, plan.chunk, width))
        total = lax.all_to_all(copies, ("tm", "state"), 0, 0, tiled=True)
        beliefs, logs = pl.pallas_call(
            lambda *refs: solve_kernel(plan, states, *refs),
            out_shape=(
                jax.ShapeDtypeStruct((frames, cells), jnp.float32),
                jax.ShapeDtypeStruct((frames, width), jnp.float32),
            ),
            in_specs=[SMEM] + [VMEM] * 5,
            out_specs=(VMEM, VMEM),
            name="solve",
        )(place, total.reshape(members, cores, plan.chunk, width), offered, other, right, entry)
        return beliefs, logs[:, 0]

    return jax.shard_map(
        per_device,
        mesh=mesh,
        in_specs=(
            P("state"),
            P("tm", None),
            P("state", "tm"),
            P("state", None, "tm"),
            P("state", None, "tm"),
            P("tm"),
        ),
        out_specs=(P("state", "tm"), P("state")),
        check_vma=False,
    )
```

time: 348 us -> 49.2 us (0.14)
  blocking collectives: 238 us -> 36.4 us
  waiting for transfers between devices: 64.7 us -> 1.22 us
  between operations: 15.6 us -> 0.65 us
  matrix products: 12.4 us -> 0 us
  Pallas kernels: 0 us -> 8.02 us
  other arithmetic: 5.31 us -> 0.02 us
  local copies, waits for them, and re-layouts: 7.07 us -> 1.98 us
    psum x6 -> x0, blocking collectives: 238 us -> none  [the longest x4 153 us: frame(): lax.psum((jnp.dot(left_rows, unscaled, precision=PRECISE), jnp.sum(unscal...]
    psum x1 -> x0, waiting for transfers between devices: 63.9 us -> none  [span_map(): lax.psum(local_terms, 'tm')]
    all_to_all x0 -> x2, blocking collectives: none -> 36.4 us  [the longest x1 18.4 us: per_device(): parts = lax.all_to_all(partial, 'tm', 0, 0, tiled=True)]
    dot_general x24 -> x0, matrix products: 12.4 us -> none  [the longest x8 7.79 us: span_map(): jnp.einsum('pw,qw->pq', pair_rows, cross_rows, precision=PRECISE)]
    pallas_call x0 -> x3, Pallas kernels: none -> 8.02 us  [the longest x1 2.96 us: per_device(): pl.pallas_call(lambda *refs: partial_kernel(plan, *refs), out_shape=jax.S...]
    reduce_sum x6 -> x1, other arithmetic: 3.62 us -> 0.02 us  [per_device(): mine = jnp.sum(parts.reshape(members, plan.chunk, width), axis=0)]
  transfers between devices with their start and end apart: 2 -> 1, of which waited for: 2 -> 1; matrix products, arithmetic and copies ran while one was open for 0% -> 0% of each run, Pallas kernels for 0% -> 0%
where the time goes in v1:
time: 49.2 us; the launch traced here: 48.8 us
  blocking collectives  36.4 us (74%)
  Pallas kernels  8.02 us (16%)
  local copies, waits for them, and re-layouts  1.98 us (4%)
  waiting for transfers between devices  1.22 us (2%)
  between operations  0.65 us (1%)
    all_to_all x1, blocking collectives, per_device(): parts = lax.all_to_all(partial, 'tm', 0, 0, tiled=True)  18.4 us
    all_to_all x1, blocking collectives, per_device(): total = lax.all_to_all(copies, ('tm', 'state'), 0, 0, tiled=True)  18.1 us
    pallas_call x1, Pallas kernels, per_device(): pl.pallas_call(lambda *refs: partial_kernel(plan, *refs), out_shape=jax.S...  2.96 us
    pallas_call x1, Pallas kernels, per_device(): pl.pallas_call(lambda *refs: solve_kernel(plan, states, *refs), out_shape...  2.74 us
    pallas_call x1, Pallas kernels, per_device(): pl.pallas_call(offer_kernel, out_shape=jax.ShapeDtypeStruct((up(rank + fr...  2.32 us
    slice x1, local copies, waits for them, and re-layouts, per_device(): return (beliefs, logs[:, 0])  1.28 us
    ppermute x1, waiting for transfers between devices, per_device(): other = lax.ppermute(offered, 'state', [(0, 1), (1, 0)])  1.22 us
  transfers between devices with their start and end apart: 1, of which 1 were waited for; matrix products, arithmetic and copies ran while one was open for 0% of the time, Pallas kernels for 0%

profile of v1, /device:TPU:0, one launch (start us, length us, event | category | flops | bytes accessed | tf_op | source)
XLA Modules:
  0.0 48.8 jit_solution(9950762371452583149)
XLA Ops:
  0.6 2.3 %offer.1.refs_1_.refs_2_ = f32[72,512]{1,0:T(8,128)} custom-call(s32[1]{0:T(128)} %bitcast.place.refs_0_, s32[4]{0:T(128)} %symbols.1, f32[512,256]{1,0:T(8,128)} %emission.1, f32[1,512]{1,0:T(1,128)} %decay.1, f32[64,512]{1,0:T(8,128)} %bitcast.11, f32[64,512]{1,0:T(8,128)} %bitcast.7), custom_call_target="tpu_custom_call" | custom-call | tf_op jit(solution)/shard_map/offer/pallas_call | solution.py:242
  3.0 0.5 %collective-permute-start = (f32[72,512]{1,0:T(8,128)}, f32[72,512]{1,0:T(8,128)S(1)}, u32[]{:S(2)}, u32[]{:S(2)}) collective-permute-start(f32[72,512]{1,0:T(8,128)} %offer.1.refs_1_.refs_2_), channel_id=1, source_target_pairs={{0,1},{1,0},{2,3},{3,2},{4,5},{5,4},{6,7},{7,6},{8,9},{9,8},{10,11... | collective-permute-start | bytes 442376 | tf_op jit(solution)/shard_map/ppermute | solution.py:249
  3.5 1.2 %collective-permute-done.refs_2_.refs_3_ = f32[72,512]{1,0:T(8,128)S(1)} collective-permute-done((f32[72,512]{1,0:T(8,128)}, f32[72,512]{1,0:T(8,128)S(1)}, u32[]{:S(2)}, u32[]{:S(2)}) %collective-permute-start) | collective-permute-done | bytes 147488 | tf_op jit(solution)/shard_map/ppermute | solution.py:249
  4.7 0.0 copy-start
  4.7 0.7 %copy-done = f32[72,512]{1,0:T(8,128)} copy-done((f32[72,512]{1,0:T(8,128)}, f32[72,512]{1,0:T(8,128)S(1)}, u32[]{:S(2)}) %copy-start) | copy-done | bytes 147480
  5.3 3.0 %partial.1 = f32[512,128]{1,0:T(8,128)} custom-call(s32[1]{0:T(128)} %bitcast.place.refs_0_, f32[72,512]{1,0:T(8,128)} %offer.1.refs_1_.refs_2_, f32[72,512]{1,0:T(8,128)} %copy-done, f32[64,512]{1,0:T(8,128)} %bitcast.12, f32[64,512]{1,0:T(8,128)} %bitcast.8, f32[1,512]{1,0:T(1,128)} %bitcast.13), custom_call_target="tpu_custom_call" | custom-call | tf_op jit(solution)/shard_map/partial/pallas_call | solution.py:250
  8.3 18.4 %all_to_all.14 = f32[16,32,128]{2,1,0:T(8,128)S(1)} all-to-all(f32[16,32,128]{2,1,0:T(8,128)} %bitcast.10), channel_id=1, replica_groups=mesh['tm'=16,'state'=2] {'tm'}, dimensions={0} | all-to-all | bytes 524288 | tf_op jit(solution)/shard_map/all_to_all | solution.py:257
  26.7 0.1 broadcast_in_dim.2
  26.8 18.1 %all_to_all.15 = f32[32,32,128]{2,1,0:T(8,128)} all-to-all(f32[32,32,128]{2,1,0:T(8,128)S(1)} %broadcast_in_dim.2), channel_id=1, replica_groups=mesh['tm'=16,'state'=2] {'tm','state'}, dimensions={0} | all-to-all | bytes 1048576 | tf_op jit(solution)/shard_map/all_to_all | solution.py:260
  44.8 2.7 %solve.1 = (f32[4,512]{1,0:T(4,128)}, f32[4,128]{1,0:T(4,128)}) custom-call(s32[1]{0:T(128)} %bitcast.place.refs_0_, f32[16,2,32,128]{3,2,1,0:T(8,128)} %bitcast.6, f32[72,512]{1,0:T(8,128)} %offer.1.refs_1_.refs_2_, f32[72,512]{1,0:T(8,128)} %copy-done, f32[64,512]{1,0:T(8,128)} %bitcast.9, f32[1,512]{1,0:T(1,128)} %bitcast.14), custom_call_target="tpu_custom_call" | custom-call | tf_op jit(solution)/shard_map/solve/pallas_call | solution.py:261
  47.5 1.3 %slice_reduce_fusion = f32[4]{0:T(128)} fusion(f32[4,128]{1,0:T(4,128)} %get-tuple-element.5), kind=kLoop, calls=%fused_computation | loop fusion | bytes 32 | tf_op jit(solution)/shard_map/slice | solution.py:271
  (1 shorter events, 0.0 us)
Async XLA Ops:
  3.0 1.7 %collective-permute-start = (f32[72,512]{1,0:T(8,128)}, f32[72,512]{1,0:T(8,128)S(1)}, u32[]{:S(2)}, u32[]{:S(2)}) collective-permute-start(f32[72,512]{1,0:T(8,128)} %offer.1.refs_1_.refs_2_), channel_id=1, source_target_pairs={{0,1},{1,0},{2,3},{3,2},{4,5},{5,4},{6,7},{7,6},{8,9},{9,8},{10,11... | collective-permute-start | bytes 442376 | tf_op jit(solution)/shard_map/ppermute | solution.py:249
  4.7 0.7 %copy-start = (f32[72,512]{1,0:T(8,128)}, f32[72,512]{1,0:T(8,128)S(1)}, u32[]{:S(2)}) copy-start(f32[72,512]{1,0:T(8,128)S(1)} %collective-permute-done.refs_2_.refs_3_) | copy-start | bytes 442372

commit v2 on v1

--- a/solution.py
+++ b/solution.py
@@ -71,45 +71,39 @@
     return jnp.concatenate(list(rows) + [jnp.zeros_like(rows[0])] * filler, axis=0)
 
 
-def both_blocks(first, own, other, rank, frames):
-    own_e = [own[rank + f : rank + f + 1] for f in range(frames)]
-    other_e = [other[rank + f : rank + f + 1] for f in range(frames)]
-    own_d = own[rank + frames : rank + frames + 1]
-    other_d = other[rank + frames : rank + frames + 1]
-    blocks = []
-    for lead in (True, False):
-        pick = first if lead else jnp.logical_not(first)
-        e = [jnp.where(pick, a, b) for a, b in zip(own_e, other_e)]
-        d = jnp.where(pick, own_d, other_d)
-        blocks.append((e, d))
-    return own_e, own_d, blocks
-
-
-def offer_kernel(place, symbols, emission, decay, left, right, out):
+def offer_kernel(place, symbols, decay, left, right, out):
     frames = symbols.shape[0]
     rank, cells = left.shape
-    pad = up(frames, 8)
-    at = lax.broadcasted_iota(jnp.int32, (pad, emission.shape[1]), 0)
-    lane = lax.broadcasted_iota(jnp.int32, (pad, emission.shape[1]), 1)
-    wanted = jnp.full(at.shape, -1, jnp.int32)
-    for f in range(frames):
-        wanted = jnp.where(at == f, symbols[f], wanted)
-    onehot = (lane == wanted).astype(jnp.float32)
-    emitted = dot_lanes(onehot, emission[...])
+    spare = out.shape[0] - rank - frames - 1
     out[:rank] = jnp.where(place[0] == 0, right[...], left[...])
-    rest = [emitted[:frames], decay[...]]
-    spare = out.shape[0] - rank - frames - 1
-    if spare:
-        rest.append(jnp.zeros((spare, cells), jnp.float32))
+    rest = [decay[...]]
+    rest += [jnp.full((1, cells), symbols[f].astype(jnp.float32)) for f in range(frames)]
+    rest += [jnp.zeros((1, cells), jnp.float32)] * spare
     out[rank:] = jnp.concatenate(rest, axis=0)
 
 
-def partial_kernel(plan, place, own_ref, other_ref, left, right, entry, out):
+def in_order(first, own, other):
+    return jnp.where(first, own, other), jnp.where(first, other, own)
+
+
+def partial_kernel(plan, place, own_ref, other_ref, emission, left, right, entry, out, seen):
     frames, rank = plan.frames, plan.rank
     first = place[0] == 0
-    own_e, own_d, ((e0, d0), (e1, d1)) = both_blocks(
-        first, own_ref[rank:], other_ref[rank:], 0, frames
-    )
+    own_d = own_ref[rank : rank + 1]
+    d0, d1 = in_order(first, own_d, other_ref[rank : rank + 1])
+    early, late = in_order(first, own_ref[rank:, :1], other_ref[rank:, :1])
+    shape = (seen.shape[0], emission.shape[1])
+    at = lax.broadcasted_iota(jnp.int32, shape, 0)
+    wanted = jnp.full(shape, -1.0, jnp.float32)
+    for f in range(frames):
+        wanted = jnp.where(at == f, early[1 + f : 2 + f], wanted)
+        wanted = jnp.where(at == frames + f, late[1 + f : 2 + f], wanted)
+    symbol = lax.broadcasted_iota(jnp.int32, shape, 1).astype(jnp.float32)
+    emitted = dot_lanes((symbol == wanted).astype(jnp.float32), emission[...])
+    seen[...] = emitted
+    e0 = [emitted[f : f + 1] for f in range(frames)]
+    e1 = [emitted[frames + f : frames + f + 1] for f in range(frames)]
+    own_e = [jnp.where(first, a, b) for a, b in zip(e0, e1)]
     left_own, right_own = left[...], right[...]
     left_late = jnp.where(first, other_ref[:rank], left_own)
     right_early = jnp.where(first, right_own, other_ref[:rank])
@@ -150,19 +144,16 @@
         out[plan.used :] = jnp.zeros((plan.rows - plan.used, out.shape[1]), jnp.float32)
 
 
-def solve_kernel(plan, states, place, total, own_ref, other_ref, right, entry, out, logs):
-    frames, rank, share, chunk = plan.frames, plan.rank, plan.share, plan.chunk
+def solve_kernel(
+    plan, states, place, mine, theirs, own_ref, other_ref, seen, right, entry, out, logs
+):
+    frames, rank, share = plan.frames, plan.rank, plan.share
     first = place[0] == 0
-    width = total.shape[3]
+    width = mine.shape[1]
     count = 2 * frames
 
     def rows(core, at, size):
-        if at % chunk == 0 and size % chunk == 0:
-            return total[at // chunk : (at + size) // chunk, core].reshape(size, width)
-        return jnp.concatenate(
-            [total[r // chunk, core, r % chunk : r % chunk + 8] for r in range(at, at + size, 8)],
-            axis=0,
-        )
+        return in_order(first, mine[at : at + size], theirs[at : at + size])[core]
 
     lane = lax.broadcasted_iota(jnp.int32, (1, width), 1)
     low = lane < rank
@@ -205,15 +196,13 @@
     mixed = jnp.sum(jnp.concatenate(level_rows, axis=0), axis=1, keepdims=True)
     levels = [base[:1]] + [base[t + 1 : t + 2] + mixed[t : t + 1] for t in range(count)]
 
-    own_e, own_d, ((e0, d0), (e1, d1)) = both_blocks(
-        first, own_ref[rank:], other_ref[rank:], 0, frames
-    )
+    d0, d1 = in_order(first, own_ref[rank : rank + 1], other_ref[rank : rank + 1])
     right_own = right[...]
     right_early = jnp.where(first, right_own, other_ref[:rank])
     belief = entry[...]
     found = []
     for t in range(count):
-        e, d = (e0[t], d0) if t < frames else (e1[t - frames], d1)
+        e, d = seen[t : t + 1], d0 if t < frames else d1
         factor = right_early if t < frames else right_own
         belief = e * (d * belief + jnp.sum(factor * cols[t], axis=0, keepdims=True))
         found.append(belief)
@@ -222,7 +211,7 @@
         before = jnp.where(first, levels[f], levels[frames + f])
         after = jnp.where(first, levels[f + 1], levels[frames + f + 1])
         out[f : f + 1] = jnp.where(first, found[f], found[frames + f]) * (states / scale)
-        logs[f : f + 1] = jnp.log(after / before)
+        logs[f] = jnp.log(after / before)[0, 0]
 
 
 def solution(mesh):
@@ -242,33 +231,36 @@
         offered = pl.pallas_call(
             offer_kernel,
             out_shape=jax.ShapeDtypeStruct((up(rank + frames + 1, 8), cells), jnp.float32),
-            in_specs=[SMEM, SMEM, VMEM, VMEM, VMEM, VMEM],
+            in_specs=[SMEM, SMEM, VMEM, VMEM, VMEM],
             out_specs=VMEM,
             name="offer",
-        )(place, symbols, emission, decay, left, right)
+        )(place, symbols, decay, left, right)
         other = lax.ppermute(offered, "state", [(0, 1), (1, 0)])
-        partial = pl.pallas_call(
+        partial, seen = pl.pallas_call(
             lambda *refs: partial_kernel(plan, *refs),
-            out_shape=jax.ShapeDtypeStruct((plan.rows, width), jnp.float32),
-            in_specs=[SMEM] + [VMEM] * 5,
-            out_specs=VMEM,
+            out_shape=(
+                jax.ShapeDtypeStruct((plan.rows, width), jnp.float32),
+                jax.ShapeDtypeStruct((up(2 * frames, 8), cells), jnp.float32),
+            ),
+            in_specs=[SMEM] + [VMEM] * 6,
+            out_specs=(VMEM, VMEM),
             name="partial",
-        )(place, offered, other, left, right, entry)
+        )(place, offered, other, emission, left, right, entry)
         parts = lax.all_to_all(partial, "tm", 0, 0, tiled=True)
-        mine = jnp.sum(parts.reshape(members, plan.chunk, width), axis=0)
-        copies = jnp.broadcast_to(mine[None], (members * cores, plan.chunk, width))
-        total = lax.all_to_all(copies, ("tm", "state"), 0, 0, tiled=True)
-        beliefs, logs = pl.pallas_call(
+        chunk = jnp.sum(parts.reshape(members, plan.chunk, width), axis=0)
+        copies = jnp.broadcast_to(chunk[None], (members, plan.chunk, width))
+        mine = lax.all_to_all(copies, "tm", 0, 0, tiled=True).reshape(plan.rows, width)
+        theirs = lax.ppermute(mine, "state", [(0, 1), (1, 0)])
+        return pl.pallas_call(
             lambda *refs: solve_kernel(plan, states, *refs),
             out_shape=(
                 jax.ShapeDtypeStruct((frames, cells), jnp.float32),
-                jax.ShapeDtypeStruct((frames, width), jnp.float32),
+                jax.ShapeDtypeStruct((frames,), jnp.float32),
             ),
-            in_specs=[SMEM] + [VMEM] * 5,
-            out_specs=(VMEM, VMEM),
+            in_specs=[SMEM] + [VMEM] * 7,
+            out_specs=(VMEM, SMEM),
             name="solve",
-        )(place, total.reshape(members, cores, plan.chunk, width), offered, other, right, entry)
-        return beliefs, logs[:, 0]
+        )(place, mine, theirs, offered, other, seen, right, entry)
 
     return jax.shard_map(
         per_device,

time: 49.2 us -> 44.8 us (0.911)
  blocking collectives: 36.4 us -> 31.2 us
  waiting for transfers between devices: 1.22 us -> 2.75 us
  local copies, waits for them, and re-layouts: 1.98 us -> 1.36 us
    all_to_all x1, blocking collectives: 18.1 us -> 12.8 us  [per_device(): lax.all_to_all(copies, 'tm', 0, 0, tiled=True).reshape(plan.rows, width)]
    ppermute x0 -> x1, waiting for transfers between devices: none -> 1.53 us  [per_device(): theirs = lax.ppermute(mine, 'state', [(0, 1), (1, 0)])]
    slice x1 -> x0, local copies, waits for them, and re-layouts: 1.28 us -> none  [per_device(): return (beliefs, logs[:, 0])]
    unnamed x2 -> x6, local copies, waits for them, and re-layouts: 0.65 us -> 1.34 us
    pallas_call x1, Pallas kernels: 2.96 us -> 3.64 us  [per_device(): pl.pallas_call(lambda *refs: partial_kernel(plan, *refs), out_shape=(jax....]
    pallas_call x1, Pallas kernels: 2.32 us -> 1.66 us  [per_device(): pl.pallas_call(offer_kernel, out_shape=jax.ShapeDtypeStruct((up(rank + fr...]
  transfers between devices with their start and end apart: 1 -> 2, of which waited for: 1 -> 2; matrix products, arithmetic and copies ran while one was open for 0% -> 0% of each run, Pallas kernels for 0% -> 0%
where the time goes in v2:
time: 44.8 us; the launch traced here: 44.5 us
  blocking collectives  31.2 us (70%)
  Pallas kernels  8.03 us (18%)
  waiting for transfers between devices  2.75 us (6%)
  local copies, waits for them, and re-layouts  1.36 us (3%)
  between operations  0.65 us (1%)
  starting transfers between devices  0.5 us (1%)
    all_to_all x1, blocking collectives, per_device(): parts = lax.all_to_all(partial, 'tm', 0, 0, tiled=True)  18.4 us
    all_to_all x1, blocking collectives, per_device(): lax.all_to_all(copies, 'tm', 0, 0, tiled=True).reshape(plan.rows, width)  12.8 us
    pallas_call x1, Pallas kernels, per_device(): pl.pallas_call(lambda *refs: partial_kernel(plan, *refs), out_shape=(jax....  3.64 us
    pallas_call x1, Pallas kernels, per_device(): pl.pallas_call(lambda *refs: solve_kernel(plan, states, *refs), out_shape...  2.73 us
    pallas_call x1, Pallas kernels, per_device(): pl.pallas_call(offer_kernel, out_shape=jax.ShapeDtypeStruct((up(rank + fr...  1.66 us
    ppermute x1, waiting for transfers between devices, per_device(): theirs = lax.ppermute(mine, 'state', [(0, 1), (1, 0)])  1.53 us
    unnamed x6, local copies, waits for them, and re-layouts  1.34 us
    ppermute x1, waiting for transfers between devices, per_device(): other = lax.ppermute(offered, 'state', [(0, 1), (1, 0)])  1.22 us
  transfers between devices with their start and end apart: 2, of which 2 were waited for; matrix products, arithmetic and copies ran while one was open for 0% of the time, Pallas kernels for 0%

profile of v2, /device:TPU:0, one launch (start us, length us, event | category | flops | bytes accessed | tf_op | source)
XLA Modules:
  0.0 44.5 jit_solution(2863259544812610721)
XLA Ops:
  0.6 1.7 %offer.1.refs_1_.refs_3_ = f32[72,512]{1,0:T(8,128)} custom-call(s32[1]{0:T(128)} %bitcast.place.refs_0_, s32[4]{0:T(128)} %symbols.1, f32[1,512]{1,0:T(1,128)} %decay.1, f32[64,512]{1,0:T(8,128)} %bitcast.11, f32[64,512]{1,0:T(8,128)} %bitcast.6), custom_call_target="tpu_custom_call" | custom-call | tf_op jit(solution)/shard_map/offer/pallas_call | solution.py:231
  2.3 0.5 %collective-permute-start = (f32[72,512]{1,0:T(8,128)}, f32[72,512]{1,0:T(8,128)S(1)}, u32[]{:S(2)}, u32[]{:S(2)}) collective-permute-start(f32[72,512]{1,0:T(8,128)} %offer.1.refs_1_.refs_3_), channel_id=1, source_target_pairs={{0,1},{1,0},{2,3},{3,2},{4,5},{5,4},{6,7},{7,6},{8,9},{9,8},{10,11... | collective-permute-start | bytes 442376 | tf_op jit(solution)/shard_map/ppermute | solution.py:238
  2.8 1.2 %collective-permute-done.refs_2_.refs_4_ = f32[72,512]{1,0:T(8,128)S(1)} collective-permute-done((f32[72,512]{1,0:T(8,128)}, f32[72,512]{1,0:T(8,128)S(1)}, u32[]{:S(2)}, u32[]{:S(2)}) %collective-permute-start) | collective-permute-done | bytes 147488 | tf_op jit(solution)/shard_map/ppermute | solution.py:238
  4.0 0.0 copy-start.1
  4.0 0.6 %copy-done.1 = f32[72,512]{1,0:T(8,128)} copy-done((f32[72,512]{1,0:T(8,128)}, f32[72,512]{1,0:T(8,128)S(1)}, u32[]{:S(2)}) %copy-start.1) | copy-done | bytes 147480
  4.7 3.6 %partial.1 = (f32[512,128]{1,0:T(8,128)}, f32[8,512]{1,0:T(8,128)}) custom-call(s32[1]{0:T(128)} %bitcast.place.refs_0_, f32[72,512]{1,0:T(8,128)} %offer.1.refs_1_.refs_3_, f32[72,512]{1,0:T(8,128)} %copy-done.1, f32[512,256]{1,0:T(8,128)} %refs_3_.1, f32[64,512]{1,0:T(8,128)} %bitcast.12, f32[64,512]{1,0:T(8,128)} %bitcast.7, f32[1,512]{1,0:T(1,128)} %bitcast.14), custom_call_target="tpu_custom_call" | custom-call | tf_op jit(solution)/shard_map/partial/pallas_call | solution.py:239
  8.3 18.4 %all_to_all.14 = f32[16,32,128]{2,1,0:T(8,128)S(1)} all-to-all(f32[16,32,128]{2,1,0:T(8,128)} %bitcast.13), channel_id=1, replica_groups=mesh['tm'=16,'state'=2] {'tm'}, dimensions={0} | all-to-all | bytes 524288 | tf_op jit(solution)/shard_map/all_to_all | solution.py:249
  26.7 12.8 %all_to_all.15 = f32[16,32,128]{2,1,0:T(8,128)S(1)} all-to-all(f32[16,32,128]{2,1,0:T(8,128)S(1)} %broadcast_in_dim.2), channel_id=1, replica_groups=mesh['tm'=16,'state'=2] {'tm'}, dimensions={0} | all-to-all | bytes 524288 | tf_op jit(solution)/shard_map/all_to_all | solution.py:252
  39.5 0.0 copy-start
  39.5 0.0 collective-permute-start.1
  39.5 1.5 %collective-permute-done.1.refs_2_ = f32[512,128]{1,0:T(8,128)S(1)} collective-permute-done((f32[512,128]{1,0:T(8,128)S(1)}, f32[512,128]{1,0:T(8,128)S(1)}, u32[]{:S(2)}, u32[]{:S(2)}) %collective-permute-start.1) | collective-permute-done | bytes 262176 | tf_op jit(solution)/shard_map/ppermute | solution.py:253
  41.1 0.0 copy-start.2
  41.1 0.0 copy-done
  41.1 0.7 %copy-done.2 = f32[512,128]{1,0:T(8,128)} copy-done((f32[512,128]{1,0:T(8,128)}, f32[512,128]{1,0:T(8,128)S(1)}, u32[]{:S(2)}) %copy-start.2) | copy-done | bytes 262168
  41.8 2.7 %solve.1 = (f32[4,512]{1,0:T(4,128)}, f32[4]{0:T(128)}) custom-call(s32[1]{0:T(128)} %bitcast.place.refs_0_, f32[512,128]{1,0:T(8,128)} %bitcast.10, f32[512,128]{1,0:T(8,128)} %copy-done.2, f32[72,512]{1,0:T(8,128)} %offer.1.refs_1_.refs_3_, f32[72,512]{1,0:T(8,128)} %copy-done.1, f32[8,512]{1,0:T(8,128)} %get-tuple-element.5.refs_5_, f32[64,512]{1,0:T(8,128)} %bitcast.8, ...), custom_call_target="tpu_custom_call" | custom-call | tf_op jit(solution)/shard_map/solve/pallas_call | solution.py:254
  (2 shorter events, 0.0 us)
Async XLA Ops:
  2.3 1.7 %collective-permute-start = (f32[72,512]{1,0:T(8,128)}, f32[72,512]{1,0:T(8,128)S(1)}, u32[]{:S(2)}, u32[]{:S(2)}) collective-permute-start(f32[72,512]{1,0:T(8,128)} %offer.1.refs_1_.refs_3_), channel_id=1, source_target_pairs={{0,1},{1,0},{2,3},{3,2},{4,5},{5,4},{6,7},{7,6},{8,9},{9,8},{10,11... | collective-permute-start | bytes 442376 | tf_op jit(solution)/shard_map/ppermute | solution.py:238
  4.0 0.7 %copy-start.1 = (f32[72,512]{1,0:T(8,128)}, f32[72,512]{1,0:T(8,128)S(1)}, u32[]{:S(2)}) copy-start(f32[72,512]{1,0:T(8,128)S(1)} %collective-permute-done.refs_2_.refs_4_) | copy-start | bytes 442372
  39.5 1.5 %copy-start = (f32[16,32,128]{2,1,0:T(8,128)}, f32[16,32,128]{2,1,0:T(8,128)S(1)}, u32[]{:S(2)}) copy-start(f32[16,32,128]{2,1,0:T(8,128)S(1)} %all_to_all.15) | copy-start | bytes 786436
  39.5 1.5 %collective-permute-start.1 = (f32[512,128]{1,0:T(8,128)S(1)}, f32[512,128]{1,0:T(8,128)S(1)}, u32[]{:S(2)}, u32[]{:S(2)}) collective-permute-start(f32[512,128]{1,0:T(8,128)S(1)} %bitcast.9), channel_id=1, source_target_pairs={{0,1},{1,0},{2,3},{3,2},{4,5},{5,4},{6,7},{7,6},{8,9},{9,8},{10,11... | collective-permute-start | bytes 786440 | tf_op jit(solution)/shard_map/ppermute | solution.py:253
  41.1 0.7 %copy-start.2 = (f32[512,128]{1,0:T(8,128)}, f32[512,128]{1,0:T(8,128)S(1)}, u32[]{:S(2)}) copy-start(f32[512,128]{1,0:T(8,128)S(1)} %collective-permute-done.1.refs_2_) | copy-start | bytes 786436

commit v3 on v2

--- a/solution.py
+++ b/solution.py
@@ -9,6 +9,10 @@
 LANES = (((1,), (1,)), ((), ()))
 VMEM = pl.BlockSpec(memory_space=pltpu.VMEM)
 SMEM = pl.BlockSpec(memory_space=pltpu.SMEM)
+
+
+def near(value):
+    return pltpu.with_memory_space_constraint(value, pltpu.VMEM)
 
 
 def up(count, step):
@@ -220,17 +224,18 @@
     assert cores == 2
 
     def per_device(symbols, emission, decay, left_factor, right_factor, initial):
-        left, right = left_factor[0], right_factor[0]
+        left, right = near(left_factor[0]), near(right_factor[0])
         frames = symbols.shape[0]
         rank, cells = left.shape
         states = members * cells
         plan = Plan(frames, rank, members)
         width = 2 * rank
         place = lax.axis_index("state").astype(jnp.int32).reshape(1)
-        entry = initial.reshape(1, cells)
+        entry = near(initial.reshape(1, cells))
+        emission = near(emission)
         offered = pl.pallas_call(
             offer_kernel,
-            out_shape=jax.ShapeDtypeStruct((up(rank + frames + 1, 8), cells), jnp.float32),
+            out_shape=pltpu.VMEM((up(rank + frames + 1, 8), cells), jnp.float32),
             in_specs=[SMEM, SMEM, VMEM, VMEM, VMEM],
             out_specs=VMEM,
             name="offer",
@@ -239,13 +244,13 @@
         partial, seen = pl.pallas_call(
             lambda *refs: partial_kernel(plan, *refs),
             out_shape=(
-                jax.ShapeDtypeStruct((plan.rows, width), jnp.float32),
-                jax.ShapeDtypeStruct((up(2 * frames, 8), cells), jnp.float32),
+                pltpu.VMEM((plan.rows, width), jnp.float32),
+                pltpu.VMEM((up(2 * frames, 8), cells), jnp.float32),
             ),
             in_specs=[SMEM] + [VMEM] * 6,
             out_specs=(VMEM, VMEM),
             name="partial",
-        )(place, offered, other, emission, left, right, entry)
+        )(place, near(offered), near(other), emission, left, right, entry)
         parts = lax.all_to_all(partial, "tm", 0, 0, tiled=True)
         chunk = jnp.sum(parts.reshape(members, plan.chunk, width), axis=0)
         copies = jnp.broadcast_to(chunk[None], (members, plan.chunk, width))
@@ -260,7 +265,7 @@
             in_specs=[SMEM] + [VMEM] * 7,
             out_specs=(VMEM, SMEM),
             name="solve",
-        )(place, mine, theirs, offered, other, seen, right, entry)
+        )(place, near(mine), near(theirs), near(offered), near(other), near(seen), right, entry)
 
     return jax.shard_map(
         per_device,

time: 44.8 us -> 41.9 us (0.935)
  Pallas kernels: 8.03 us -> 4.01 us
  local copies, waits for them, and re-layouts: 1.36 us -> 2.87 us
    pallas_call x2, Pallas kernels: 5.3 us -> 2.48 us  [the longest x1 1.67 us: per_device(): pl.pallas_call(lambda *refs: partial_kernel(plan, *refs), out_shape=(pltp...]
    unnamed x6 -> x8, local copies, waits for them, and re-layouts: 1.34 us -> 2.85 us
    pallas_call x1, Pallas kernels: 2.73 us -> 1.53 us  [per_device(): pl.pallas_call(lambda *refs: solve_kernel(plan, states, *refs), out_shape...]
where the time goes in v3:
time: 41.9 us; the launch traced here: 41.6 us
  blocking collectives  31 us (74%)
  Pallas kernels  4.01 us (10%)
  local copies, waits for them, and re-layouts  2.87 us (7%)
  waiting for transfers between devices  2.54 us (6%)
  between operations  0.67 us (2%)
  starting transfers between devices  0.56 us (1%)
    all_to_all x1, blocking collectives, per_device(): parts = lax.all_to_all(partial, 'tm', 0, 0, tiled=True)  18.2 us
    all_to_all x1, blocking collectives, per_device(): lax.all_to_all(copies, 'tm', 0, 0, tiled=True).reshape(plan.rows, width)  12.8 us
    unnamed x8, local copies, waits for them, and re-layouts  2.85 us
    pallas_call x1, Pallas kernels, per_device(): pl.pallas_call(lambda *refs: partial_kernel(plan, *refs), out_shape=(pltp...  1.67 us
    ppermute x1, waiting for transfers between devices, per_device(): theirs = lax.ppermute(mine, 'state', [(0, 1), (1, 0)])  1.53 us
    pallas_call x1, Pallas kernels, per_device(): pl.pallas_call(lambda *refs: solve_kernel(plan, states, *refs), out_shape...  1.53 us
    ppermute x1, waiting for transfers between devices, per_device(): other = lax.ppermute(offered, 'state', [(0, 1), (1, 0)])  1.01 us
  transfers between devices with their start and end apart: 2, of which 2 were waited for; matrix products, arithmetic and copies ran while one was open for 0% of the time, Pallas kernels for 0%

profile of v3, /device:TPU:0, one launch (start us, length us, event | category | flops | bytes accessed | tf_op | source)
XLA Modules:
  0.0 41.6 jit_solution(16731519629584850117)
XLA Ops:
  0.6 0.0 copy-start
  0.6 0.9 %copy-done = f32[1,64,512]{2,1,0:T(8,128)S(1)} copy-done((f32[1,64,512]{2,1,0:T(8,128)S(1)}, f32[1,64,512]{2,1,0:T(8,128)}, u32[]{:S(2)}) %copy-start) | copy-done | bytes 131096
  1.5 0.0 copy-start.2
  1.5 0.9 %copy-done.2 = f32[1,64,512]{2,1,0:T(8,128)S(1)} copy-done((f32[1,64,512]{2,1,0:T(8,128)S(1)}, f32[1,64,512]{2,1,0:T(8,128)}, u32[]{:S(2)}) %copy-start.2) | copy-done | bytes 131096
  2.4 0.0 copy-start.3
  2.4 0.8 %offer.1.refs_1_.refs_3_ = f32[72,512]{1,0:T(8,128)S(1)} custom-call(s32[1]{0:T(128)} %bitcast.place.refs_0_, s32[4]{0:T(128)} %symbols.1, f32[1,512]{1,0:T(1,128)} %decay.1, f32[64,512]{1,0:T(8,128)S(1)} %bitcast.11, f32[64,512]{1,0:T(8,128)S(1)} %bitcast.6), custom_call_target="tpu_custom_call" | custom-call | tf_op jit(solution)/shard_map/offer/pallas_call | solution.py:236
  3.3 0.6 %collective-permute-start = (f32[72,512]{1,0:T(8,128)S(1)}, f32[72,512]{1,0:T(8,128)S(1)}, u32[]{:S(2)}, u32[]{:S(2)}) collective-permute-start(f32[72,512]{1,0:T(8,128)S(1)} %offer.1.refs_1_.refs_3_), channel_id=1, source_target_pairs={{0,1},{1,0},{2,3},{3,2},{4,5},{5,4},{6,7},{7,6},{8,9},{9,8},{10,11... | collective-permute-start | bytes 442376 | tf_op jit(solution)/shard_map/ppermute | solution.py:243
  3.8 1.0 %collective-permute-done.refs_2_.refs_4_ = f32[72,512]{1,0:T(8,128)S(1)} collective-permute-done((f32[72,512]{1,0:T(8,128)S(1)}, f32[72,512]{1,0:T(8,128)S(1)}, u32[]{:S(2)}, u32[]{:S(2)}) %collective-permute-start) | collective-permute-done | bytes 147488 | tf_op jit(solution)/shard_map/ppermute | solution.py:243
  4.8 0.0 copy-done.3
  4.8 0.0 copy-start.1
  4.8 1.0 %copy-done.1 = f32[512,256]{1,0:T(8,128)S(1)} copy-done((f32[512,256]{1,0:T(8,128)S(1)}, f32[512,256]{1,0:T(8,128)}, u32[]{:S(2)}) %copy-start.1) | copy-done | bytes 524312
  5.9 1.7 %partial.1 = (f32[512,128]{1,0:T(8,128)S(1)}, f32[8,512]{1,0:T(8,128)S(1)}) custom-call(s32[1]{0:T(128)} %bitcast.place.refs_0_, f32[72,512]{1,0:T(8,128)S(1)} %offer.1.refs_1_.refs_3_, f32[72,512]{1,0:T(8,128)S(1)} %collective-permute-done.refs_2_.refs_4_, f32[512,256]{1,0:T(8,128)S(1)} %copy-done.1, f32[64,512]{1,0:T(8,128)S(1)} %bitcast.12, ...), custom_call_target="tpu_custom_call" | custom-call | tf_op jit(solution)/shard_map/partial/pallas_call | solution.py:244
  7.5 18.2 %all_to_all.14 = f32[16,32,128]{2,1,0:T(8,128)S(1)} all-to-all(f32[16,32,128]{2,1,0:T(8,128)S(1)} %bitcast.13), channel_id=1, replica_groups=mesh['tm'=16,'state'=2] {'tm'}, dimensions={0} | all-to-all | bytes 524288 | tf_op jit(solution)/shard_map/all_to_all | solution.py:254
  25.8 12.8 %all_to_all.15 = f32[16,32,128]{2,1,0:T(8,128)S(1)} all-to-all(f32[16,32,128]{2,1,0:T(8,128)S(1)} %broadcast_in_dim.2), channel_id=1, replica_groups=mesh['tm'=16,'state'=2] {'tm'}, dimensions={0} | all-to-all | bytes 524288 | tf_op jit(solution)/shard_map/all_to_all | solution.py:257
  38.6 0.0 collective-permute-start.1
  38.6 1.5 %collective-permute-done.1.refs_2_ = f32[512,128]{1,0:T(8,128)S(1)} collective-permute-done((f32[512,128]{1,0:T(8,128)S(1)}, f32[512,128]{1,0:T(8,128)S(1)}, u32[]{:S(2)}, u32[]{:S(2)}) %collective-permute-start.1) | collective-permute-done | bytes 262176 | tf_op jit(solution)/shard_map/ppermute | solution.py:258
  40.1 1.5 %solve.1 = (f32[4,512]{1,0:T(4,128)}, f32[4]{0:T(128)}) custom-call(s32[1]{0:T(128)} %bitcast.place.refs_0_, f32[512,128]{1,0:T(8,128)S(1)} %bitcast.10, f32[512,128]{1,0:T(8,128)S(1)} %collective-permute-done.1.refs_2_, f32[72,512]{1,0:T(8,128)S(1)} %offer.1.refs_1_.refs_3_, f32[72,512]{1,0:T(8,128)S(1)} %collective-permute-done.refs_2_.refs_4_, ...), custom_call_target="tpu_custom_call" | custom-call | tf_op jit(solution)/shard_map/solve/pallas_call | solution.py:259
  (2 shorter events, 0.0 us)
Async XLA Ops:
  0.6 0.9 %copy-start = (f32[1,64,512]{2,1,0:T(8,128)S(1)}, f32[1,64,512]{2,1,0:T(8,128)}, u32[]{:S(2)}) copy-start(f32[1,64,512]{2,1,0:T(8,128)} %param.10) | copy-start | bytes 393220
  1.5 0.9 %copy-start.2 = (f32[1,64,512]{2,1,0:T(8,128)S(1)}, f32[1,64,512]{2,1,0:T(8,128)}, u32[]{:S(2)}) copy-start(f32[1,64,512]{2,1,0:T(8,128)} %param.9) | copy-start | bytes 393220
  2.4 2.4 %copy-start.3 = (f32[512]{0:T(512)S(1)}, f32[512]{0:T(512)}, u32[]{:S(2)}) copy-start(f32[512]{0:T(512)} %param.11) | copy-start | bytes 6148
  3.3 1.6 %collective-permute-start = (f32[72,512]{1,0:T(8,128)S(1)}, f32[72,512]{1,0:T(8,128)S(1)}, u32[]{:S(2)}, u32[]{:S(2)}) collective-permute-start(f32[72,512]{1,0:T(8,128)S(1)} %offer.1.refs_1_.refs_3_), channel_id=1, source_target_pairs={{0,1},{1,0},{2,3},{3,2},{4,5},{5,4},{6,7},{7,6},{8,9},{9,8},{10,11... | collective-permute-start | bytes 442376 | tf_op jit(solution)/shard_map/ppermute | solution.py:243
  4.8 1.0 %copy-start.1 = (f32[512,256]{1,0:T(8,128)S(1)}, f32[512,256]{1,0:T(8,128)}, u32[]{:S(2)}) copy-start(f32[512,256]{1,0:T(8,128)} %refs_3_.1) | copy-start | bytes 1572868
  38.6 1.5 %collective-permute-start.1 = (f32[512,128]{1,0:T(8,128)S(1)}, f32[512,128]{1,0:T(8,128)S(1)}, u32[]{:S(2)}, u32[]{:S(2)}) collective-permute-start(f32[512,128]{1,0:T(8,128)S(1)} %bitcast.9), channel_id=1, source_target_pairs={{0,1},{1,0},{2,3},{3,2},{4,5},{5,4},{6,7},{7,6},{8,9},{9,8},{10,11... | collective-permute-start | bytes 786440 | tf_op jit(solution)/shard_map/ppermute | solution.py:258
